TPU v7x, 32 devices: a whole 2x2x4 slice. The times are simulated.
32 devices in a mesh: gx: 4 (over y, core), gy: 4 (over z), gz: 2 (over x).
Axes of the slice: x: 2, y: 2, z: 4, core: 2. Of those that a mesh axis runs over, the one named last changes fastest.
Arguments:
- positions: float32 [3, 4, 32, 2, 128], P(None, 'gx', ('gy', 'gz')), may hold values from 0 to 3
- velocities: float32 [3, 4, 32, 2, 128], P(None, 'gx', ('gy', 'gz')), may hold values from -6 to 6
- bead_keys: int32 [4, 32, 2, 128], P('gx', ('gy', 'gz')), may hold values from 0 to 1073741823
- counts: int32 [4, 32, 2], P('gx', ('gy', 'gz')), may hold values from 64 to 128
Outputs:
- half_kick: float32 [3, 4, 32, 2, 128], P(None, 'gx', 'gy', 'gz')
Inputs may be any that keep to these rules, and one draw needn't show every extreme that they name: Slots from counts of a tile on are padding and take no part. `bead_keys`: the lowest bit of a key names the bead type, 0 water and 1 polymer.
All inputs are finite; a program needn't handle non-finite values.
Results may differ from a plain program's by a relative error of at most 0.0003.
Values sent between devices are 32-bit elements; how exact they have to be, the bound alone decides.
A program may use at most 64 MiB of HBM per device.

v0:
```python
import jax
import jax.numpy as jnp
from jax import lax
from jax.sharding import PartitionSpec as P

SIDE = 3


soft_radius = 0.05
friction = 4.5
noise_amplitude = 15.0
like_repulsion = 25.0
unlike_extra = 15.0
kick_scale = 0.02
root_twelve = 3.4641016151377544


def padded(x, sides, width):
    for axis, dim in sides:
        count, length = (lax.axis_size(axis), x.shape[dim])
        up = [(i, (i + 1) % count) for i in range(count)]
        down = [(j, i) for i, j in up]
        last = lax.slice_in_dim(x, length - width, length, axis=dim)
        leading = lax.slice_in_dim(x, 0, width, axis=dim)
        before = lax.ppermute(last, axis, up)
        after = lax.ppermute(leading, axis, down)
        x = jnp.concatenate([before, x, after], axis=dim)
    return x


def pair_noise(first_keys, second_keys):
    hashed = (first_keys ^ second_keys) * 1103515245 + (first_keys + second_keys) * 12345
    hashed = hashed ^ hashed >> 15 & 131071
    hashed = hashed * 747796405
    hashed = hashed ^ hashed >> 13 & 524287
    fraction = (hashed >> 7 & 16777215).astype(jnp.float32) * (1.0 / 16777216.0)
    return root_twelve * (fraction - 0.5)


def pair_forces(own_motion, own_keys, other_motion, other_keys, other_counts, displace):
    slot_index = lax.broadcasted_iota(jnp.int32, other_keys.shape, 1)
    present = (slot_index < other_counts[:, None]).astype(jnp.float32)
    separation = [
        own_motion[component][:, :, None]
        - (other_motion[component][:, None, :] + displace[component])
        for component in range(3)
    ]
    squared = (
        separation[0] * separation[0]
        + separation[1] * separation[1]
        + separation[2] * separation[2]
    )
    distance = jnp.sqrt(squared)
    weight = jnp.maximum(1.0 - distance, 0.0) * present[:, None, :]
    inverse = 1.0 / jnp.maximum(distance, soft_radius)
    approach = separation[0] * (own_motion[3][:, :, None] - other_motion[3][:, None, :])
    approach = approach + separation[1] * (own_motion[4][:, :, None] - other_motion[4][:, None, :])
    approach = approach + separation[2] * (own_motion[5][:, :, None] - other_motion[5][:, None, :])
    approach = approach * inverse
    first_keys = own_keys[:, :, None]
    second_keys = other_keys[:, None, :]
    random_pair = pair_noise(first_keys, second_keys)
    repulsion = like_repulsion + unlike_extra * ((first_keys ^ second_keys) & 1).astype(jnp.float32)
    strength = (
        repulsion * weight
        - friction * weight * weight * approach
        + noise_amplitude * weight * random_pair
    ) * inverse
    return jnp.stack([jnp.sum(strength * part, axis=2) for part in separation])


def wrap_layer(field, along):
    last = lax.slice_in_dim(field, field.shape[along] - 1, field.shape[along], axis=along)
    first = lax.slice_in_dim(field, 0, 1, axis=along)
    return jnp.concatenate([last, field, first], axis=along)


def tile_kick(padded_motion, padded_keys, padded_counts):
    size_x = padded_keys.shape[0] - 2
    size_y = padded_keys.shape[1] - 2
    size_z = padded_keys.shape[2] - 2
    slots = padded_keys.shape[3]
    tiles = size_x * size_y * size_z
    own_motion = padded_motion[:, 1 : size_x + 1, 1 : size_y + 1, 1 : size_z + 1, :].reshape(
        6, tiles, slots
    )
    own_keys = padded_keys[1 : size_x + 1, 1 : size_y + 1, 1 : size_z + 1, :].reshape(tiles, slots)
    own_counts = padded_counts[1 : size_x + 1, 1 : size_y + 1, 1 : size_z + 1].reshape(tiles)
    anchor = jnp.int32(0)

    def add_offset(offset, summed):
        offset = jnp.asarray(offset).astype(jnp.int32)
        off_x = offset // 9
        off_y = offset // 3 % 3
        off_z = offset % 3
        other_motion = lax.dynamic_slice(
            padded_motion, (anchor, off_x, off_y, off_z, anchor), (6, size_x, size_y, size_z, slots)
        ).reshape(6, tiles, slots)
        other_keys = lax.dynamic_slice(
            padded_keys, (off_x, off_y, off_z, anchor), (size_x, size_y, size_z, slots)
        ).reshape(tiles, slots)
        other_counts = lax.dynamic_slice(
            padded_counts, (off_x, off_y, off_z), (size_x, size_y, size_z)
        ).reshape(tiles)
        displace = SIDE * (jnp.stack([off_x, off_y, off_z]) - 1).astype(jnp.float32)
        return summed + pair_forces(
            own_motion, own_keys, other_motion, other_keys, other_counts, displace
        )

    summed = lax.fori_loop(0, 27, add_offset, jnp.zeros((3, tiles, slots), jnp.float32))
    slot_index = lax.broadcasted_iota(jnp.int32, (tiles, slots), 1)
    occupied = (slot_index < own_counts[:, None]).astype(jnp.float32)
    kick = kick_scale * summed * occupied[None]
    return kick.reshape(3, size_x, size_y, size_z, slots)


def on_device(positions, velocities, bead_keys, counts):
    motion = jnp.concatenate([positions, velocities], axis=0)
    padded_motion = padded(motion, (("gx", 1), (("gy", "gz"), 2)), 1)
    padded_keys, padded_counts = (
        padded(bead_keys, (("gx", 0), (("gy", "gz"), 1)), 1),
        padded(counts, (("gx", 0), (("gy", "gz"), 1)), 1),
    )
    padded_motion = wrap_layer(padded_motion, 3)
    padded_keys = wrap_layer(padded_keys, 2)
    padded_counts = wrap_layer(padded_counts, 2)
    kick = tile_kick(padded_motion, padded_keys, padded_counts)
    return lax.all_to_all(kick, "gz", split_axis=3, concat_axis=2, tiled=True)


def solution(mesh):
    in_specs = (
        P(None, "gx", ("gy", "gz"), None, None),
        P(None, "gx", ("gy", "gz"), None, None),
        P("gx", ("gy", "gz"), None, None),
        P("gx", ("gy", "gz"), None),
    )
    out_specs = P(None, "gx", "gy", "gz", None)
    return jax.shard_map(
        on_device, mesh=mesh, in_specs=in_specs, out_specs=out_specs, check_vma=False
    )
```

profile of v0, /device:TPU:0, one launch (start us, length us, event | category | flops | bytes accessed | tf_op | source)
XLA Modules:
  0.0 178.3 jit_solution(17720979427389668819)
XLA Ops:
  1.3 2.0 %collective-permute-start.5 = (f32[6,1,4,2,128]{4,3,2,1,0:T(2,128)S(1)}, f32[6,1,4,2,128]{4,3,2,1,0:T(2,128)S(1)}, u32[]{:S(2)}, u32[]{:S(2)}) collective-permute-start(f32[6,1,4,2,128]{4,3,2,1,0:T(2,128)S(1)} %constant_dynamic-update-slice_fusion.3), channel_id=1, source_target_pairs={{8,0},{16,8},{24,16},{0,24},{9,1},{17,9},{25,17},{1,25},{10,2},{18... | collective-permute-start | bytes 73736 | tf_op jit(solution)/shard_map/ppermute | solution.py:26
  7.1 2.2 %collective-permute-start.10 = (s32[3,1,2]{1,2,0:T(2,128)S(1)}, s32[3,1,2]{1,2,0:T(2,128)S(1)}, u32[]{:S(2)}, u32[]{:S(2)}) collective-permute-start(s32[3,1,2]{1,2,0:T(2,128)S(1)} %get-tuple-element.305), channel_id=1, source_target_pairs={{0,1},{1,2},{2,3},{3,4},{4,5},{5,6},{6,7},{7,0},{8,9},{9,10},{10,1... | collective-permute-start | bytes 80 | tf_op jit(solution)/shard_map/ppermute | solution.py:25
  9.4 4.6 %collective-permute-done.10 = s32[3,1,2]{1,2,0:T(2,128)S(1)} collective-permute-done((s32[3,1,2]{1,2,0:T(2,128)S(1)}, s32[3,1,2]{1,2,0:T(2,128)S(1)}, u32[]{:S(2)}, u32[]{:S(2)}) %collective-permute-start.10) | collective-permute-done | bytes 56 | tf_op jit(solution)/shard_map/ppermute | solution.py:25
  14.0 2.0 %collective-permute-start.11 = (s32[3,1,2]{1,2,0:T(2,128)S(1)}, s32[3,1,2]{1,2,0:T(2,128)S(1)}, u32[]{:S(2)}, u32[]{:S(2)}) collective-permute-start(s32[3,1,2]{1,2,0:T(2,128)S(1)} %get-tuple-element.306), channel_id=1, source_target_pairs={{1,0},{2,1},{3,2},{4,3},{5,4},{6,5},{7,6},{0,7},{9,8},{10,9},{11,1... | collective-permute-start | bytes 80 | tf_op jit(solution)/shard_map/ppermute | solution.py:26
  17.8 4.8 %collective-permute-start.3 = (s32[3,1,2,128]{3,2,1,0:T(2,128)S(1)}, s32[3,1,2,128]{3,2,1,0:T(2,128)S(1)}, u32[]{:S(2)}, u32[]{:S(2)}) collective-permute-start(s32[3,1,2,128]{3,2,1,0:T(2,128)S(1)} %get-tuple-element.302), channel_id=1, source_target_pairs={{1,0},{2,1},{3,2},{4,3},{5,4},{6,5},{7,6},{0,7},{9,8},{10,9},{11,1... | collective-permute-start | bytes 9224 | tf_op jit(solution)/shard_map/ppermute | solution.py:26
  24.2 4.8 %collective-permute-start.7 = (f32[6,3,1,2,128]{4,3,2,1,0:T(2,128)S(1)}, f32[6,3,1,2,128]{4,3,2,1,0:T(2,128)S(1)}, u32[]{:S(2)}, u32[]{:S(2)}) collective-permute-start(f32[6,3,1,2,128]{4,3,2,1,0:T(2,128)S(1)} %get-tuple-element.298), channel_id=1, source_target_pairs={{1,0},{2,1},{3,2},{4,3},{5,4},{6,5},{7,6},{0,7},{9,8},{10,9},{11,1... | collective-permute-start | bytes 55304 | tf_op jit(solution)/shard_map/ppermute | solution.py:26
  31.0 140.4 %while.17 = (s32[]{:T(128)}, f32[3,8,128]{2,1,0:T(8,128)S(1)}, s32[1,4,2,128]{3,2,1,0:T(2,128)S(1)}, s32[3,6,4,128]{3,2,1,0:T(4,128)S(1)}, f32[6,8,128]{2,1,0:T(...) while((s32[]{:T(128)}, f32[3,8,128]{2,1,0:T(8,128)S(1)}, ...), condition=%wide.region_4.5_spmd.clone, body=%wide.region_0.4_spmd.clone.sunk | while | flops 7747640 | bytes 222095 | solution.py:110
  34.2 2.0 %fusion.35 = (f32[8,128]{1,0:T(8,128)S(1)}, f32[8,128]{1,0:T(8,128)S(1)}, f32[8,128]{1,0:T(8,128)S(1)}) fusion(f32[8,128]{1,0:T(8,128)S(1)} %bitcast.82, f32[8,128]{1,0:T(8,128)S(1)} %get-tuple-element.372, f32[8,128]{1,0:T(8,128)S(1)} %bitcast.83, f32[8,128]{1,0:T(8,128)S(1)} %get-tuple-element.374, f32[8,128]{1,0:T(8,128)S(1)} %bitcast.79, ...), kind=kLoop, calls=%fused_computation.27.clone.1 | loop fusion | flops 7730176 | bytes 73728 | tf_op jit(solution)/shard_map/while/body/eval_jaxpr/reduce_sum | solution.py:69
  39.4 2.0 %fusion.35 = (f32[8,128]{1,0:T(8,128)S(1)}, f32[8,128]{1,0:T(8,128)S(1)}, f32[8,128]{1,0:T(8,128)S(1)}) fusion(f32[8,128]{1,0:T(8,128)S(1)} %bitcast.82, f32[8,128]{1,0:T(8,128)S(1)} %get-tuple-element.372, f32[8,128]{1,0:T(8,128)S(1)} %bitcast.83, f32[8,128]{1,0:T(8,128)S(1)} %get-tuple-element.374, f32[8,128]{1,0:T(8,128)S(1)} %bitcast.79, ...), kind=kLoop, calls=%fused_computation.27.clone.1 | loop fusion | flops 7730176 | bytes 73728 | tf_op jit(solution)/shard_map/while/body/eval_jaxpr/reduce_sum | solution.py:69
  44.6 2.0 %fusion.35 = (f32[8,128]{1,0:T(8,128)S(1)}, f32[8,128]{1,0:T(8,128)S(1)}, f32[8,128]{1,0:T(8,128)S(1)}) fusion(f32[8,128]{1,0:T(8,128)S(1)} %bitcast.82, f32[8,128]{1,0:T(8,128)S(1)} %get-tuple-element.372, f32[8,128]{1,0:T(8,128)S(1)} %bitcast.83, f32[8,128]{1,0:T(8,128)S(1)} %get-tuple-element.374, f32[8,128]{1,0:T(8,128)S(1)} %bitcast.79, ...), kind=kLoop, calls=%fused_computation.27.clone.1 | loop fusion | flops 7730176 | bytes 73728 | tf_op jit(solution)/shard_map/while/body/eval_jaxpr/reduce_sum | solution.py:69
  65.4 2.0 %fusion.35 = (f32[8,128]{1,0:T(8,128)S(1)}, f32[8,128]{1,0:T(8,128)S(1)}, f32[8,128]{1,0:T(8,128)S(1)}) fusion(f32[8,128]{1,0:T(8,128)S(1)} %bitcast.82, f32[8,128]{1,0:T(8,128)S(1)} %get-tuple-element.372, f32[8,128]{1,0:T(8,128)S(1)} %bitcast.83, f32[8,128]{1,0:T(8,128)S(1)} %get-tuple-element.374, f32[8,128]{1,0:T(8,128)S(1)} %bitcast.79, ...), kind=kLoop, calls=%fused_computation.27.clone.1 | loop fusion | flops 7730176 | bytes 73728 | tf_op jit(solution)/shard_map/while/body/eval_jaxpr/reduce_sum | solution.py:69
  70.6 2.0 %fusion.35 = (f32[8,128]{1,0:T(8,128)S(1)}, f32[8,128]{1,0:T(8,128)S(1)}, f32[8,128]{1,0:T(8,128)S(1)}) fusion(f32[8,128]{1,0:T(8,128)S(1)} %bitcast.82, f32[8,128]{1,0:T(8,128)S(1)} %get-tuple-element.372, f32[8,128]{1,0:T(8,128)S(1)} %bitcast.83, f32[8,128]{1,0:T(8,128)S(1)} %get-tuple-element.374, f32[8,128]{1,0:T(8,128)S(1)} %bitcast.79, ...), kind=kLoop, calls=%fused_computation.27.clone.1 | loop fusion | flops 7730176 | bytes 73728 | tf_op jit(solution)/shard_map/while/body/eval_jaxpr/reduce_sum | solution.py:69
  75.8 2.0 %fusion.35 = (f32[8,128]{1,0:T(8,128)S(1)}, f32[8,128]{1,0:T(8,128)S(1)}, f32[8,128]{1,0:T(8,128)S(1)}) fusion(f32[8,128]{1,0:T(8,128)S(1)} %bitcast.82, f32[8,128]{1,0:T(8,128)S(1)} %get-tuple-element.372, f32[8,128]{1,0:T(8,128)S(1)} %bitcast.83, f32[8,128]{1,0:T(8,128)S(1)} %get-tuple-element.374, f32[8,128]{1,0:T(8,128)S(1)} %bitcast.79, ...), kind=kLoop, calls=%fused_computation.27.clone.1 | loop fusion | flops 7730176 | bytes 73728 | tf_op jit(solution)/shard_map/while/body/eval_jaxpr/reduce_sum | solution.py:69
  81.0 2.0 %fusion.35 = (f32[8,128]{1,0:T(8,128)S(1)}, f32[8,128]{1,0:T(8,128)S(1)}, f32[8,128]{1,0:T(8,128)S(1)}) fusion(f32[8,128]{1,0:T(8,128)S(1)} %bitcast.82, f32[8,128]{1,0:T(8,128)S(1)} %get-tuple-element.372, f32[8,128]{1,0:T(8,128)S(1)} %bitcast.83, f32[8,128]{1,0:T(8,128)S(1)} %get-tuple-element.374, f32[8,128]{1,0:T(8,128)S(1)} %bitcast.79, ...), kind=kLoop, calls=%fused_computation.27.clone.1 | loop fusion | flops 7730176 | bytes 73728 | tf_op jit(solution)/shard_map/while/body/eval_jaxpr/reduce_sum | solution.py:69
  86.2 2.0 %fusion.35 = (f32[8,128]{1,0:T(8,128)S(1)}, f32[8,128]{1,0:T(8,128)S(1)}, f32[8,128]{1,0:T(8,128)S(1)}) fusion(f32[8,128]{1,0:T(8,128)S(1)} %bitcast.82, f32[8,128]{1,0:T(8,128)S(1)} %get-tuple-element.372, f32[8,128]{1,0:T(8,128)S(1)} %bitcast.83, f32[8,128]{1,0:T(8,128)S(1)} %get-tuple-element.374, f32[8,128]{1,0:T(8,128)S(1)} %bitcast.79, ...), kind=kLoop, calls=%fused_computation.27.clone.1 | loop fusion | flops 7730176 | bytes 73728 | tf_op jit(solution)/shard_map/while/body/eval_jaxpr/reduce_sum | solution.py:69
  91.4 2.0 %fusion.35 = (f32[8,128]{1,0:T(8,128)S(1)}, f32[8,128]{1,0:T(8,128)S(1)}, f32[8,128]{1,0:T(8,128)S(1)}) fusion(f32[8,128]{1,0:T(8,128)S(1)} %bitcast.82, f32[8,128]{1,0:T(8,128)S(1)} %get-tuple-element.372, f32[8,128]{1,0:T(8,128)S(1)} %bitcast.83, f32[8,128]{1,0:T(8,128)S(1)} %get-tuple-element.374, f32[8,128]{1,0:T(8,128)S(1)} %bitcast.79, ...), kind=kLoop, calls=%fused_computation.27.clone.1 | loop fusion | flops 7730176 | bytes 73728 | tf_op jit(solution)/shard_map/while/body/eval_jaxpr/reduce_sum | solution.py:69
  96.6 2.0 %fusion.35 = (f32[8,128]{1,0:T(8,128)S(1)}, f32[8,128]{1,0:T(8,128)S(1)}, f32[8,128]{1,0:T(8,128)S(1)}) fusion(f32[8,128]{1,0:T(8,128)S(1)} %bitcast.82, f32[8,128]{1,0:T(8,128)S(1)} %get-tuple-element.372, f32[8,128]{1,0:T(8,128)S(1)} %bitcast.83, f32[8,128]{1,0:T(8,128)S(1)} %get-tuple-element.374, f32[8,128]{1,0:T(8,128)S(1)} %bitcast.79, ...), kind=kLoop, calls=%fused_computation.27.clone.1 | loop fusion | flops 7730176 | bytes 73728 | tf_op jit(solution)/shard_map/while/body/eval_jaxpr/reduce_sum | solution.py:69
  101.8 2.0 %fusion.35 = (f32[8,128]{1,0:T(8,128)S(1)}, f32[8,128]{1,0:T(8,128)S(1)}, f32[8,128]{1,0:T(8,128)S(1)}) fusion(f32[8,128]{1,0:T(8,128)S(1)} %bitcast.82, f32[8,128]{1,0:T(8,128)S(1)} %get-tuple-element.372, f32[8,128]{1,0:T(8,128)S(1)} %bitcast.83, f32[8,128]{1,0:T(8,128)S(1)} %get-tuple-element.374, f32[8,128]{1,0:T(8,128)S(1)} %bitcast.79, ...), kind=kLoop, calls=%fused_computation.27.clone.1 | loop fusion | flops 7730176 | bytes 73728 | tf_op jit(solution)/shard_map/while/body/eval_jaxpr/reduce_sum | solution.py:69
  107.0 2.0 %fusion.35 = (f32[8,128]{1,0:T(8,128)S(1)}, f32[8,128]{1,0:T(8,128)S(1)}, f32[8,128]{1,0:T(8,128)S(1)}) fusion(f32[8,128]{1,0:T(8,128)S(1)} %bitcast.82, f32[8,128]{1,0:T(8,128)S(1)} %get-tuple-element.372, f32[8,128]{1,0:T(8,128)S(1)} %bitcast.83, f32[8,128]{1,0:T(8,128)S(1)} %get-tuple-element.374, f32[8,128]{1,0:T(8,128)S(1)} %bitcast.79, ...), kind=kLoop, calls=%fused_computation.27.clone.1 | loop fusion | flops 7730176 | bytes 73728 | tf_op jit(solution)/shard_map/while/body/eval_jaxpr/reduce_sum | solution.py:69
  112.2 2.0 %fusion.35 = (f32[8,128]{1,0:T(8,128)S(1)}, f32[8,128]{1,0:T(8,128)S(1)}, f32[8,128]{1,0:T(8,128)S(1)}) fusion(f32[8,128]{1,0:T(8,128)S(1)} %bitcast.82, f32[8,128]{1,0:T(8,128)S(1)} %get-tuple-element.372, f32[8,128]{1,0:T(8,128)S(1)} %bitcast.83, f32[8,128]{1,0:T(8,128)S(1)} %get-tuple-element.374, f32[8,128]{1,0:T(8,128)S(1)} %bitcast.79, ...), kind=kLoop, calls=%fused_computation.27.clone.1 | loop fusion | flops 7730176 | bytes 73728 | tf_op jit(solution)/shard_map/while/body/eval_jaxpr/reduce_sum | solution.py:69
  117.4 2.0 %fusion.35 = (f32[8,128]{1,0:T(8,128)S(1)}, f32[8,128]{1,0:T(8,128)S(1)}, f32[8,128]{1,0:T(8,128)S(1)}) fusion(f32[8,128]{1,0:T(8,128)S(1)} %bitcast.82, f32[8,128]{1,0:T(8,128)S(1)} %get-tuple-element.372, f32[8,128]{1,0:T(8,128)S(1)} %bitcast.83, f32[8,128]{1,0:T(8,128)S(1)} %get-tuple-element.374, f32[8,128]{1,0:T(8,128)S(1)} %bitcast.79, ...), kind=kLoop, calls=%fused_computation.27.clone.1 | loop fusion | flops 7730176 | bytes 73728 | tf_op jit(solution)/shard_map/while/body/eval_jaxpr/reduce_sum | solution.py:69
  164.2 2.0 %fusion.35 = (f32[8,128]{1,0:T(8,128)S(1)}, f32[8,128]{1,0:T(8,128)S(1)}, f32[8,128]{1,0:T(8,128)S(1)}) fusion(f32[8,128]{1,0:T(8,128)S(1)} %bitcast.82, f32[8,128]{1,0:T(8,128)S(1)} %get-tuple-element.372, f32[8,128]{1,0:T(8,128)S(1)} %bitcast.83, f32[8,128]{1,0:T(8,128)S(1)} %get-tuple-element.374, f32[8,128]{1,0:T(8,128)S(1)} %bitcast.79, ...), kind=kLoop, calls=%fused_computation.27.clone.1 | loop fusion | flops 7730176 | bytes 73728 | tf_op jit(solution)/shard_map/while/body/eval_jaxpr/reduce_sum | solution.py:69
  169.4 2.0 %fusion.35 = (f32[8,128]{1,0:T(8,128)S(1)}, f32[8,128]{1,0:T(8,128)S(1)}, f32[8,128]{1,0:T(8,128)S(1)}) fusion(f32[8,128]{1,0:T(8,128)S(1)} %bitcast.82, f32[8,128]{1,0:T(8,128)S(1)} %get-tuple-element.372, f32[8,128]{1,0:T(8,128)S(1)} %bitcast.83, f32[8,128]{1,0:T(8,128)S(1)} %get-tuple-element.374, f32[8,128]{1,0:T(8,128)S(1)} %bitcast.79, ...), kind=kLoop, calls=%fused_computation.27.clone.1 | loop fusion | flops 7730176 | bytes 73728 | tf_op jit(solution)/shard_map/while/body/eval_jaxpr/reduce_sum | solution.py:69
  171.5 6.2 %all_to_all.18 = f32[3,1,4,2,128]{4,2,0,1,3:T(4,128)S(1)} all-to-all(f32[3,1,4,2,128]{4,2,0,1,3:T(4,128)S(1)} %copy.24), channel_id=1, replica_groups=mesh['gx'=4,'gy'=4,'gz'=2] {'gz'}, dimensions={3} | all-to-all | bytes 24576 | tf_op jit(solution)/shard_map/all_to_all | solution.py:128
  (332 shorter events, 115.6 us)
Async XLA Ops:
  0.0 0.7 copy-start
  0.7 2.6 %copy-start.1 = (s32[1,4,2]{1,2,0:T(2,128)S(1)}, s32[1,4,2]{1,2,0:T(2,128)}, u32[]{:S(2)}) copy-start(s32[1,4,2]{1,2,0:T(2,128)} %param.9) | copy-start | bytes 100
  0.7 4.3 %copy-start.2 = (s32[1,4,2,128]{3,2,1,0:T(2,128)S(1)}, s32[1,4,2,128]{3,2,1,0:T(2,128)}, u32[]{:S(2)}) copy-start(s32[1,4,2,128]{3,2,1,0:T(2,128)} %param.8) | copy-start | bytes 12292
  0.7 23.4 %collective-permute-start.4 = (f32[6,1,4,2,128]{4,3,2,1,0:T(2,128)S(1)}, f32[6,1,4,2,128]{4,3,2,1,0:T(2,128)S(1)}, u32[]{:S(2)}, u32[]{:S(2)}) collective-permute-start(f32[6,1,4,2,128]{4,3,2,1,0:T(2,128)S(1)} %constant_dynamic-update-slice_fusion.3), channel_id=1, source_target_pairs={{0,8},{8,16},{16,24},{24,0},{1,9},{9,17},{17,25},{25,1},{2,10},{10... | collective-permute-start | bytes 73736 | tf_op jit(solution)/shard_map/ppermute | solution.py:25
  1.3 22.8 %collective-permute-start.5 = (f32[6,1,4,2,128]{4,3,2,1,0:T(2,128)S(1)}, f32[6,1,4,2,128]{4,3,2,1,0:T(2,128)S(1)}, u32[]{:S(2)}, u32[]{:S(2)}) collective-permute-start(f32[6,1,4,2,128]{4,3,2,1,0:T(2,128)S(1)} %constant_dynamic-update-slice_fusion.3), channel_id=1, source_target_pairs={{8,0},{16,8},{24,16},{0,24},{9,1},{17,9},{25,17},{1,25},{10,2},{18... | collective-permute-start | bytes 73736 | tf_op jit(solution)/shard_map/ppermute | solution.py:26
  3.3 3.0 %collective-permute-start.8 = (s32[1,4,2]{1,2,0:T(2,128)S(1)}, s32[1,4,2]{1,2,0:T(2,128)S(1)}, u32[]{:S(2)}, u32[]{:S(2)}) collective-permute-start(s32[1,4,2]{1,2,0:T(2,128)S(1)} %copy-done.1), channel_id=1, source_target_pairs={{0,8},{8,16},{16,24},{24,0},{1,9},{9,17},{17,25},{25,1},{2,10},{10... | collective-permute-start | bytes 104 | tf_op jit(solution)/shard_map/ppermute | solution.py:25
  3.9 3.2 %collective-permute-start.9 = (s32[1,4,2]{1,2,0:T(2,128)S(1)}, s32[1,4,2]{1,2,0:T(2,128)S(1)}, u32[]{:S(2)}, u32[]{:S(2)}) collective-permute-start(s32[1,4,2]{1,2,0:T(2,128)S(1)} %copy-done.1), channel_id=1, source_target_pairs={{8,0},{16,8},{24,16},{0,24},{9,1},{17,9},{25,17},{1,25},{10,2},{18... | collective-permute-start | bytes 104 | tf_op jit(solution)/shard_map/ppermute | solution.py:26
  5.0 12.6 %collective-permute-start = (s32[1,4,2,128]{3,2,1,0:T(2,128)S(1)}, s32[1,4,2,128]{3,2,1,0:T(2,128)S(1)}, u32[]{:S(2)}, u32[]{:S(2)}) collective-permute-start(s32[1,4,2,128]{3,2,1,0:T(2,128)S(1)} %copy-done.2), channel_id=1, source_target_pairs={{0,8},{8,16},{16,24},{24,0},{1,9},{9,17},{17,25},{25,1},{2,10},{10... | collective-permute-start | bytes 12296 | tf_op jit(solution)/shard_map/ppermute | solution.py:25
  6.3 11.4 %collective-permute-start.1 = (s32[1,4,2,128]{3,2,1,0:T(2,128)S(1)}, s32[1,4,2,128]{3,2,1,0:T(2,128)S(1)}, u32[]{:S(2)}, u32[]{:S(2)}) collective-permute-start(s32[1,4,2,128]{3,2,1,0:T(2,128)S(1)} %copy-done.2), channel_id=1, source_target_pairs={{8,0},{16,8},{24,16},{0,24},{9,1},{17,9},{25,17},{1,25},{10,2},{18... | collective-permute-start | bytes 12296 | tf_op jit(solution)/shard_map/ppermute | solution.py:26
  7.1 6.8 %collective-permute-start.10 = (s32[3,1,2]{1,2,0:T(2,128)S(1)}, s32[3,1,2]{1,2,0:T(2,128)S(1)}, u32[]{:S(2)}, u32[]{:S(2)}) collective-permute-start(s32[3,1,2]{1,2,0:T(2,128)S(1)} %get-tuple-element.305), channel_id=1, source_target_pairs={{0,1},{1,2},{2,3},{3,4},{4,5},{5,6},{6,7},{7,0},{8,9},{9,10},{10,1... | collective-permute-start | bytes 80 | tf_op jit(solution)/shard_map/ppermute | solution.py:25
  14.0 3.6 %collective-permute-start.11 = (s32[3,1,2]{1,2,0:T(2,128)S(1)}, s32[3,1,2]{1,2,0:T(2,128)S(1)}, u32[]{:S(2)}, u32[]{:S(2)}) collective-permute-start(s32[3,1,2]{1,2,0:T(2,128)S(1)} %get-tuple-element.306), channel_id=1, source_target_pairs={{1,0},{2,1},{3,2},{4,3},{5,4},{6,5},{7,6},{0,7},{9,8},{10,9},{11,1... | collective-permute-start | bytes 80 | tf_op jit(solution)/shard_map/ppermute | solution.py:26
  17.7 6.3 %collective-permute-start.2 = (s32[3,1,2,128]{3,2,1,0:T(2,128)S(1)}, s32[3,1,2,128]{3,2,1,0:T(2,128)S(1)}, u32[]{:S(2)}, u32[]{:S(2)}) collective-permute-start(s32[3,1,2,128]{3,2,1,0:T(2,128)S(1)} %get-tuple-element.301), channel_id=1, source_target_pairs={{0,1},{1,2},{2,3},{3,4},{4,5},{5,6},{6,7},{7,0},{8,9},{9,10},{10,1... | collective-permute-start | bytes 9224 | tf_op jit(solution)/shard_map/ppermute | solution.py:25
  17.8 6.3 %collective-permute-start.3 = (s32[3,1,2,128]{3,2,1,0:T(2,128)S(1)}, s32[3,1,2,128]{3,2,1,0:T(2,128)S(1)}, u32[]{:S(2)}, u32[]{:S(2)}) collective-permute-start(s32[3,1,2,128]{3,2,1,0:T(2,128)S(1)} %get-tuple-element.302), channel_id=1, source_target_pairs={{1,0},{2,1},{3,2},{4,3},{5,4},{6,5},{7,6},{0,7},{9,8},{10,9},{11,1... | collective-permute-start | bytes 9224 | tf_op jit(solution)/shard_map/ppermute | solution.py:26
  24.1 6.6 %collective-permute-start.6 = (f32[6,3,1,2,128]{4,3,2,1,0:T(2,128)S(1)}, f32[6,3,1,2,128]{4,3,2,1,0:T(2,128)S(1)}, u32[]{:S(2)}, u32[]{:S(2)}) collective-permute-start(f32[6,3,1,2,128]{4,3,2,1,0:T(2,128)S(1)} %get-tuple-element.297), channel_id=1, source_target_pairs={{0,1},{1,2},{2,3},{3,4},{4,5},{5,6},{6,7},{7,0},{8,9},{9,10},{10,1... | collective-permute-start | bytes 55304 | tf_op jit(solution)/shard_map/ppermute | solution.py:25
  24.2 6.5 %collective-permute-start.7 = (f32[6,3,1,2,128]{4,3,2,1,0:T(2,128)S(1)}, f32[6,3,1,2,128]{4,3,2,1,0:T(2,128)S(1)}, u32[]{:S(2)}, u32[]{:S(2)}) collective-permute-start(f32[6,3,1,2,128]{4,3,2,1,0:T(2,128)S(1)} %get-tuple-element.298), channel_id=1, source_target_pairs={{1,0},{2,1},{3,2},{4,3},{5,4},{6,5},{7,6},{0,7},{9,8},{10,9},{11,1... | collective-permute-start | bytes 55304 | tf_op jit(solution)/shard_map/ppermute | solution.py:26
where the time goes:
time: 179 us; the launch traced here: 178 us
  other arithmetic  111 us (62%)
  local copies, waits for them, and re-layouts  27.4 us (15%)
  starting transfers between devices  19.6 us (11%)
  waiting for transfers between devices  9.66 us (5%)
  blocking collectives  6.18 us (3%)
  loops' own time  3.84 us (2%)
    reduce_sum x27, other arithmetic, pair_forces(): return jnp.stack([jnp.sum(strength * part, axis=2) for part in separation])  54.1 us
    add x27, other arithmetic, pair_forces(): other_motion[component][:, None, :] + displace[component]  52.6 us
    slice x27, local copies, waits for them, and re-layouts, pair_forces(): displace[component]  18.1 us
    ppermute x6, starting transfers between devices, padded(): after = lax.ppermute(leading, axis, down)  15.5 us
    ppermute x6, waiting for transfers between devices, padded(): before = lax.ppermute(last, axis, up)  8.07 us
    all_to_all x1, blocking collectives, on_device(): return lax.all_to_all(kick, 'gz', split_axis=3, concat_axis=2, tiled=True)  6.18 us
    dynamic_slice x54, local copies, waits for them, and re-layouts, add_offset(): lax.dynamic_slice(padded_counts, (off_x, off_y, off_z), (size_x, size_y,...  4.73 us
    ppermute x6, starting transfers between devices, padded(): before = lax.ppermute(last, axis, up)  4.1 us
  transfers between devices with their start and end apart: 12, of which 5 were waited for; matrix products, arithmetic and copies ran while one was open for 0% of the time, Pallas kernels for 0%

commit v1 on v0

v1 whole, which is shorter than its diff:
```python
import functools

import jax
import jax.numpy as jnp
from jax import lax
from jax.experimental import pallas as pl
from jax.experimental.pallas import tpu as pltpu
from jax.sharding import PartitionSpec as P

SIDE = 3.0

soft_radius = 0.05
friction = 4.5
noise_amplitude = 15.0
like_repulsion = 25.0
unlike_extra = 15.0
kick_scale = 0.02
root_twelve = 3.4641016151377544

FAR = 1.0e9
ROWS = 8
GROUP = 64
MESH = pl.DeviceIdType.MESH


def gather_kernel(sizes, pos_ref, vel_ref, key_ref, count_ref, all_ref, packed, send, recv, edge_send, edge_recv, local):
    nx, ny, nz, block_y, tiles_z = sizes
    gx, gy, gz = lax.axis_index("gx"), lax.axis_index("gy"), lax.axis_index("gz")
    slots = pos_ref.shape[-1]
    top = nz * block_y + 1
    barrier = pltpu.get_barrier_semaphore()

    def target(e, group, member):
        return (lax.rem(gx + e + nx, nx), lax.rem(gy + group + ny, ny), lax.rem(member + nz, nz))

    steps = (-1, 0, 1)
    for e in steps:
        for r in range(nz):
            if e or r:
                pl.semaphore_signal(barrier, inc=1, device_id=target(e, 0, gz + r), device_id_type=MESH)
        pl.semaphore_signal(barrier, inc=1, device_id=target(e, -1, nz - 1), device_id_type=MESH)
        pl.semaphore_signal(barrier, inc=1, device_id=target(e, 1, 0), device_id_type=MESH)

    lane = lax.broadcasted_iota(jnp.int32, (1, slots), 1)
    for y in range(block_y):
        for z in range(tiles_z):
            present = lane < count_ref[0, y, z]
            key = key_ref[0, y, pl.ds(z, 1), :]
            rows = [jnp.where(present, pos_ref[c, 0, y, pl.ds(z, 1), :], FAR) for c in range(3)]
            rows += [vel_ref[c, 0, y, pl.ds(z, 1), :] * friction for c in range(3)]
            rows += [(key >> 15).astype(jnp.float32), (key & 32767).astype(jnp.float32)]
            packed[y, z] = jnp.concatenate(rows, axis=0)

    def group_copy(e, r, slot_of):
        return pltpu.make_async_remote_copy(
            src_ref=packed,
            dst_ref=all_ref.at[1 - e, pl.ds(1 + slot_of * block_y, block_y)],
            send_sem=send.at[e + 1, r],
            recv_sem=recv.at[e + 1, r],
            device_id=target(e, 0, gz + r),
            device_id_type=MESH,
        )

    def edge_copy(e, side, member):
        first = side == 0
        return pltpu.make_async_remote_copy(
            src_ref=packed.at[pl.ds(0 if first else block_y - 1, 1)],
            dst_ref=all_ref.at[1 - e, pl.ds(top if first else 0, 1)],
            send_sem=edge_send.at[side, e + 1, member],
            recv_sem=edge_recv.at[side, e + 1],
            device_id=target(e, -1 if first else 1, member),
            device_id_type=MESH,
        )

    ends = jnp.where(gz == 0, 1, 0) + jnp.where(gz == nz - 1, 1, 0)
    pl.semaphore_wait(barrier, 3 * nz - 1 + 3 * nz * ends)

    for e in (-1, 1, 0):
        for r in range(nz):
            if e or r:
                group_copy(e, r, gz).start()

    def edges(side, act):
        for e in (-1, 1, 0):
            for member in range(nz):
                act(edge_copy(e, side, member))

    @pl.when(gz == 0)
    def _():
        edges(0, lambda c: c.start())

    @pl.when(gz == nz - 1)
    def _():
        edges(1, lambda c: c.start())

    mine = pltpu.make_async_copy(packed, all_ref.at[1, pl.ds(1 + gz * block_y, block_y)], local)
    mine.start()
    mine.wait()
    for e in steps:
        for r in range(nz):
            if e or r:
                copy = group_copy(e, r, lax.rem(gz - r + nz, nz))
                copy.wait_recv()
                copy.wait_send()
        for side in range(2):
            edge_copy(e, side, 0).wait_recv()

    @pl.when(gz == 0)
    def _():
        edges(0, lambda c: c.wait_send())

    @pl.when(gz == nz - 1)
    def _():
        edges(1, lambda c: c.wait_send())


def pair_kernel(sizes, all_ref, out_ref, jbuf, column, forces):
    tiles_z, out_y, out_z = sizes
    slots = all_ref.shape[-1]
    gz = lax.axis_index("gz")
    row = lax.broadcasted_iota(jnp.int32, (ROWS, slots), 0)
    lane = lax.broadcasted_iota(jnp.int32, (ROWS, slots), 1)
    low = jnp.where(row < 3, -1.0, -3.0e38)
    high = jnp.where(row < 3, SIDE + 1.0, 3.0e38)

    layers = (0, None) if tiles_z == 2 else (-1, 0, 1)
    shell = [
        (dx, dy, dz)
        for dx in (-1, 0, 1)
        for dy in (-1, 0, 1)
        for dz in layers
        if (dx, dy, dz) != (0, 0, 0)
    ]
    n = len(shell)
    padded_n = -(-n // 8) * 8
    bits = (n * slots - 1).bit_length()
    lane_bits = (slots - 1).bit_length()
    upper = (
        lax.broadcasted_iota(jnp.int32, (slots, slots), 0)
        < lax.broadcasted_iota(jnp.int32, (slots, slots), 1)
    ).astype(jnp.bfloat16)
    below = (
        lax.broadcasted_iota(jnp.int32, (padded_n, padded_n), 1)
        < lax.broadcasted_iota(jnp.int32, (padded_n, padded_n), 0)
    ).astype(jnp.bfloat16)
    flat = lax.broadcasted_iota(jnp.int32, (padded_n, slots), 0) * slots + lax.broadcasted_iota(
        jnp.int32, (padded_n, slots), 1
    )

    def shift(x, bit):
        if bit < lane_bits:
            amount = 1 << bit
            rolled = pltpu.roll(x, slots - amount, 1)
            after = jnp.concatenate([rolled[ROWS:], rolled[:ROWS]], axis=0)
            lanes = lax.broadcasted_iota(jnp.int32, x.shape, 1)
            return jnp.where(lanes < slots - amount, rolled, after)
        cut = ROWS << (bit - lane_bits)
        return jnp.concatenate([x[cut:], x[:cut]], axis=0)

    def one_tile(tile, carry):
        y = tile // out_z
        zz = tile % out_z
        z = gz * out_z + zz
        own = all_ref[1, y + 1, z]
        pieces, masks = [], []
        for dx, dy, dz in shell:
            if dz is None:
                v = all_ref[1 + dx, y + 1 + dy, 1 - z]
                shift_z = jnp.where(v < 0.5 * SIDE, SIDE, -SIDE)
            else:
                v = all_ref[1 + dx, y + 1 + dy, lax.rem(z + dz + tiles_z, tiles_z)]
                shift_z = SIDE * dz
            move = jnp.where(row == 0, SIDE * dx, jnp.where(row == 1, SIDE * dy, jnp.where(row == 2, shift_z, 0.0)))
            v = v + move
            inside = jnp.where((v > low) & (v < high), 1.0, 0.0)
            masks.append(jnp.min(inside, axis=0, keepdims=True))
            pieces.append(v)
        masks += [jnp.zeros((1, slots), jnp.float32)] * (padded_n - n)
        mask = jnp.concatenate(masks, axis=0)
        half = mask.astype(jnp.bfloat16)
        before = jnp.dot(half, upper, preferred_element_type=jnp.float32)
        per_row = jnp.sum(mask, axis=1, keepdims=True)
        rows_before = jnp.dot(
            below,
            jnp.broadcast_to(per_row, (padded_n, slots)).astype(jnp.bfloat16),
            preferred_element_type=jnp.float32,
        )
        total = jnp.sum(mask).astype(jnp.int32)
        distance_left = jnp.where(mask > 0.5, flat - (before + rows_before).astype(jnp.int32), 0)
        x = jnp.concatenate(pieces, axis=0)
        s = jnp.concatenate(
            [jnp.broadcast_to(distance_left[k : k + 1], (ROWS, slots)) for k in range(n)], axis=0
        )
        for bit in range(bits):
            near = shift(s, bit)
            take = (near & (1 << bit)) != 0
            leaves = (s & (1 << bit)) != 0
            x = jnp.where(take, shift(x, bit), x)
            s = jnp.where(take, near, jnp.where(leaves, 0, s))
        jbuf[0] = own
        for k in range(n):
            jbuf[1 + k] = jnp.where(lane + k * slots < total, x[k * ROWS : (k + 1) * ROWS], FAR)
        blocks = 1 + (total + slots - 1) // slots

        column[:, :ROWS] = jnp.transpose(own)
        count = jnp.sum(jnp.where(own[0:1] < 0.5 * FAR, 1.0, 0.0)).astype(jnp.int32)
        groups = (count + GROUP - 1) // GROUP

        def one_group(g, carry):
            base = pl.multiple_of(g * GROUP, GROUP)

            def wide(c):
                return jnp.broadcast_to(column[pl.ds(base, GROUP), c : c + 1], (GROUP, slots))

            xi = [wide(c) for c in range(6)]
            klo = wide(7).astype(jnp.int32)
            ki = wide(6).astype(jnp.int32) * 32768 + klo
            ai = ki * 12345
            ti = (klo & 1).astype(jnp.float32) * unlike_extra - 0.5 * unlike_extra

            def one_block(b, acc):
                def other(c):
                    return jbuf[b, pl.ds(c, 1), :]

                sep = [xi[c] - other(c) for c in range(3)]
                squared = sep[0] * sep[0] + sep[1] * sep[1] + sep[2] * sep[2]
                distance = squared * lax.rsqrt(jnp.maximum(squared, 1e-30))
                inverse = lax.rsqrt(jnp.maximum(squared, soft_radius * soft_radius))
                weight = jnp.maximum(1.0 - distance, 0.0)
                dot = (
                    sep[0] * (xi[3] - other(3))
                    + sep[1] * (xi[4] - other(4))
                    + sep[2] * (xi[5] - other(5))
                )
                lo = other(7).astype(jnp.int32)
                kj = other(6).astype(jnp.int32) * 32768 + lo
                tj = 1.0 - 2.0 * (lo & 1).astype(jnp.float32)
                hashed = (ki ^ kj) * 1103515245 + (ai + kj * 12345)
                hashed = hashed ^ lax.shift_right_logical(hashed, 15)
                hashed = hashed * 747796405
                hashed = hashed ^ lax.shift_right_logical(hashed, 13)
                fraction = (lax.shift_right_logical(hashed, 7) & 16777215).astype(jnp.float32)
                unit = noise_amplitude * root_twelve
                push = (
                    fraction * (unit / 16777216.0)
                    + (like_repulsion + 0.5 * unlike_extra - 0.5 * unit)
                    + ti * tj
                )
                scaled = weight * inverse
                strength = scaled * (push - scaled * dot)
                return tuple(acc[c] + strength * sep[c] for c in range(3))

            zero = jnp.zeros((GROUP, slots), jnp.float32)
            acc = lax.fori_loop(0, blocks, one_block, (zero, zero, zero))
            lanes = lax.broadcasted_iota(jnp.int32, (GROUP, slots), 1)
            sums = [jnp.sum(a, axis=1, keepdims=True) for a in acc]
            forces[pl.ds(base, GROUP), :] = jnp.where(
                lanes == 0, sums[0], jnp.where(lanes == 1, sums[1], sums[2])
            )
            return carry

        lax.fori_loop(0, groups, one_group, 0)
        turned = jnp.transpose(forces[...])
        kick = jnp.where(lane[:3] < count, kick_scale * turned[:3], 0.0)
        for c in range(3):
            out_ref[c, 0, y, pl.ds(zz, 1), :] = kick[c : c + 1]
        return carry

    lax.fori_loop(0, out_y * out_z, one_tile, 0)


def on_device(nx, ny, nz, positions, velocities, bead_keys, counts):
    _, _, block_y, tiles_z, slots = positions.shape
    out_y, out_z = block_y * nz, tiles_z // nz
    span = out_y + 2
    gathered = pl.pallas_call(
        functools.partial(gather_kernel, (nx, ny, nz, block_y, tiles_z)),
        out_shape=jax.ShapeDtypeStruct((3, span, tiles_z, ROWS, slots), jnp.float32),
        in_specs=[pl.BlockSpec(memory_space=pltpu.VMEM)] * 3 + [pl.BlockSpec(memory_space=pltpu.SMEM)],
        out_specs=pl.BlockSpec(memory_space=pltpu.VMEM),
        scratch_shapes=[
            pltpu.VMEM((block_y, tiles_z, ROWS, slots), jnp.float32),
            pltpu.SemaphoreType.DMA((3, nz)),
            pltpu.SemaphoreType.DMA((3, nz)),
            pltpu.SemaphoreType.DMA((2, 3, nz)),
            pltpu.SemaphoreType.DMA((2, 3)),
            pltpu.SemaphoreType.DMA,
        ],
        compiler_params=pltpu.CompilerParams(collective_id=0, has_side_effects=True),
        name="gather_tiles",
    )(positions, velocities, bead_keys, counts)
    shells = 17 if tiles_z == 2 else 26
    return pl.pallas_call(
        functools.partial(pair_kernel, (tiles_z, out_y, out_z)),
        out_shape=jax.ShapeDtypeStruct((3, 1, out_y, out_z, slots), jnp.float32),
        in_specs=[pl.BlockSpec(memory_space=pltpu.VMEM)],
        out_specs=pl.BlockSpec(memory_space=pltpu.VMEM),
        scratch_shapes=[
            pltpu.VMEM((1 + shells, ROWS, slots), jnp.float32),
            pltpu.VMEM((slots, slots), jnp.float32),
            pltpu.VMEM((slots, slots), jnp.float32),
        ],
        name="pair_kicks",
    )(gathered)


def solution(mesh):
    in_specs = (
        P(None, "gx", ("gy", "gz"), None, None),
        P(None, "gx", ("gy", "gz"), None, None),
        P("gx", ("gy", "gz"), None, None),
        P("gx", ("gy", "gz"), None),
    )
    out_specs = P(None, "gx", "gy", "gz", None)
    nx, ny, nz = mesh.shape["gx"], mesh.shape["gy"], mesh.shape["gz"]
    return jax.shard_map(
        functools.partial(on_device, nx, ny, nz),
        mesh=mesh,
        in_specs=in_specs,
        out_specs=out_specs,
        check_vma=False,
    )
```

time: 179 us -> 31.1 us (0.17)
  other arithmetic: 111 us -> 0 us
  Pallas kernels: 0 us -> 29.7 us
  local copies, waits for them, and re-layouts: 27.4 us -> 1.34 us
  starting transfers between devices: 19.6 us -> 0 us
  waiting for transfers between devices: 9.66 us -> 0 us
  blocking collectives: 6.18 us -> 0 us
  loops' own time: 3.84 us -> 0 us
    reduce_sum x27 -> x0, other arithmetic: 54.1 us -> none  [pair_forces(): return jnp.stack([jnp.sum(strength * part, axis=2) for part in separation])]
    add x54 -> x0, other arithmetic: 52.7 us -> none  [the longest x27 52.6 us: pair_forces(): other_motion[component][:, None, :] + displace[component]]
    pallas_call x0 -> x2, Pallas kernels: none -> 29.7 us  [the longest x1 18.2 us: on_device(): pl.pallas_call(functools.partial(pair_kernel, (tiles_z, out_y, out_z)), o...]
    ppermute x12 -> x0, starting transfers between devices: 19.6 us -> none  [the longest x6 15.5 us: padded(): after = lax.ppermute(leading, axis, down)]
    slice x32 -> x0, local copies, waits for them, and re-layouts: 18.3 us -> none  [the longest x27 18.1 us: pair_forces(): displace[component]]
    ppermute x12 -> x0, waiting for transfers between devices: 9.66 us -> none  [the longest x6 8.07 us: padded(): before = lax.ppermute(last, axis, up)]
    all_to_all x1 -> x0, blocking collectives: 6.18 us -> none  [on_device(): return lax.all_to_all(kick, 'gz', split_axis=3, concat_axis=2, tiled=True)]
    dynamic_slice x81 -> x0, local copies, waits for them, and re-layouts: 5.14 us -> none  [the longest x54 4.73 us: add_offset(): lax.dynamic_slice(padded_counts, (off_x, off_y, off_z), (size_x, size_y,...]
  transfers between devices with their start and end apart: 12 -> 0, of which waited for: 5 -> 0; matrix products, arithmetic and copies ran while one was open for 0% -> 0% of each run, Pallas kernels for 0% -> 0%
where the time goes in v1:
time: 31.1 us; the launch traced here: 31 us
  Pallas kernels  29.7 us (95%)
  local copies, waits for them, and re-layouts  1.34 us (4%)
    pallas_call x1, Pallas kernels, on_device(): pl.pallas_call(functools.partial(pair_kernel, (tiles_z, out_y, out_z)), o...  18.2 us
    pallas_call x1, Pallas kernels, on_device(): pl.pallas_call(functools.partial(gather_kernel, (nx, ny, nz, block_y, til...  11.4 us
    unnamed x1, local copies, waits for them, and re-layouts  1.34 us

profile of v1, /device:TPU:0, one launch (start us, length us, event | category | flops | bytes accessed | tf_op | source)
XLA Modules:
  0.0 31.0 jit_solution(3017597313880727538)
XLA Ops:
  0.0 1.3 %copy.5.count_ref = s32[1,4,2]{2,1,0:T(4,128)} copy(s32[1,4,2]{1,2,0:T(2,128)} %param.7) | data formatting | bytes 64 | tf_op args[3]
  1.3 11.4 %gather_tiles.1.all_ref = f32[3,10,2,8,128]{4,3,2,1,0:T(8,128)} custom-call(f32[3,1,4,2,128]{4,3,2,1,0:T(2,128)} %pos_ref.1, f32[3,1,4,2,128]{4,3,2,1,0:T(2,128)} %vel_ref.1, s32[1,4,2,128]{3,2,1,0:T(2,128)} %key_ref.1, s32[1,4,2]{2,1,0:T(4,128)} %copy.5.count_ref), custom_call_target="tpu_custom_call" | custom-call | tf_op jit(solution)/shard_map/gather_tiles/pallas_call | solution.py:276
  12.8 18.2 %pair_kicks.1 = f32[3,1,8,1,128]{4,3,2,1,0:T(1,128)} custom-call(f32[3,10,2,8,128]{4,3,2,1,0:T(8,128)} %gather_tiles.1.all_ref), custom_call_target="tpu_custom_call" | custom-call | tf_op jit(solution)/shard_map/pair_kicks/pallas_call | solution.py:293

commit v2 on v1

--- a/solution.py
+++ b/solution.py
@@ -44,7 +44,7 @@
     lane = lax.broadcasted_iota(jnp.int32, (1, slots), 1)
     for y in range(block_y):
         for z in range(tiles_z):
-            present = lane < count_ref[0, y, z]
+            present = lane < count_ref[0, z, y]
             key = key_ref[0, y, pl.ds(z, 1), :]
             rows = [jnp.where(present, pos_ref[c, 0, y, pl.ds(z, 1), :], FAR) for c in range(3)]
             rows += [vel_ref[c, 0, y, pl.ds(z, 1), :] * friction for c in range(3)]
@@ -114,96 +114,114 @@
         edges(1, lambda c: c.wait_send())
 
 
-def pair_kernel(sizes, all_ref, out_ref, jbuf, column, forces):
+def shell_of(tiles_z):
+    layers = (0, None) if tiles_z == 2 else (-1, 0, 1)
+    offsets = [(dx, dy, dz) for dx in (-1, 0, 1) for dy in (-1, 0, 1) for dz in layers]
+    return [offset for offset in offsets if offset != (0, 0, 0)]
+
+
+def pair_kernel(sizes, all_ref, out_ref, jbuf, column, forces, masks, places, sources, moved, limits):
     tiles_z, out_y, out_z = sizes
     slots = all_ref.shape[-1]
+    tiles = out_y * out_z
     gz = lax.axis_index("gz")
     row = lax.broadcasted_iota(jnp.int32, (ROWS, slots), 0)
     lane = lax.broadcasted_iota(jnp.int32, (ROWS, slots), 1)
     low = jnp.where(row < 3, -1.0, -3.0e38)
     high = jnp.where(row < 3, SIDE + 1.0, 3.0e38)
-
-    layers = (0, None) if tiles_z == 2 else (-1, 0, 1)
-    shell = [
-        (dx, dy, dz)
-        for dx in (-1, 0, 1)
-        for dy in (-1, 0, 1)
-        for dz in layers
-        if (dx, dy, dz) != (0, 0, 0)
-    ]
+    shell = shell_of(tiles_z)
     n = len(shell)
-    padded_n = -(-n // 8) * 8
-    bits = (n * slots - 1).bit_length()
+    padded_n = masks.shape[0] // tiles
+
+    def candidate(k, y, z):
+        dx, dy, dz = shell[k]
+        if dz is None:
+            v = all_ref[1 + dx, y + 1 + dy, 1 - z]
+            shift_z = jnp.where(v < 0.5 * SIDE, SIDE, -SIDE)
+        else:
+            v = all_ref[1 + dx, y + 1 + dy, lax.rem(z + dz + tiles_z, tiles_z)]
+            shift_z = SIDE * dz
+        return v + jnp.where(
+            row == 0, SIDE * dx, jnp.where(row == 1, SIDE * dy, jnp.where(row == 2, shift_z, 0.0))
+        )
+
+    def mark(tile, carry):
+        y, z = tile // out_z, gz * out_z + tile % out_z
+        rows = []
+        for k in range(n):
+            v = candidate(k, y, z)
+            inside = jnp.where((v > low) & (v < high), 1.0, 0.0)
+            rows.append(jnp.min(inside, axis=0, keepdims=True))
+        rows += [jnp.zeros((1, slots), jnp.float32)] * (padded_n - n)
+        masks[pl.ds(pl.multiple_of(tile * padded_n, 8), padded_n), :] = jnp.concatenate(rows, axis=0)
+        return carry
+
+    lax.fori_loop(0, tiles, mark, 0)
+
+    def square(size, test):
+        i = lax.broadcasted_iota(jnp.int32, (size, size), 0)
+        j = lax.broadcasted_iota(jnp.int32, (size, size), 1)
+        return jnp.where(test(i, j), 1.0, 0.0).astype(jnp.bfloat16)
+
+    height = tiles * padded_n
+    mask = masks[...]
+    half = mask.astype(jnp.bfloat16)
+    rank = jnp.dot(half, square(slots, lambda i, j: i < j), preferred_element_type=jnp.float32)
+    inside = jnp.dot(half, jnp.ones((slots, slots), jnp.bfloat16), preferred_element_type=jnp.float32)
+    start = jnp.concatenate(
+        [
+            jnp.dot(
+                square(padded_n, lambda i, j: j < i),
+                inside[t * padded_n : (t + 1) * padded_n].astype(jnp.bfloat16),
+                preferred_element_type=jnp.float32,
+            )
+            for t in range(tiles)
+        ],
+        axis=0,
+    ).astype(jnp.int32)
+    inside = inside.astype(jnp.int32)
+    lanes = lax.broadcasted_iota(jnp.int32, (height, slots), 1)
+    left = jnp.where(mask > 0.5, lanes - rank.astype(jnp.int32), 0)
     lane_bits = (slots - 1).bit_length()
-    upper = (
-        lax.broadcasted_iota(jnp.int32, (slots, slots), 0)
-        < lax.broadcasted_iota(jnp.int32, (slots, slots), 1)
-    ).astype(jnp.bfloat16)
-    below = (
-        lax.broadcasted_iota(jnp.int32, (padded_n, padded_n), 1)
-        < lax.broadcasted_iota(jnp.int32, (padded_n, padded_n), 0)
-    ).astype(jnp.bfloat16)
-    flat = lax.broadcasted_iota(jnp.int32, (padded_n, slots), 0) * slots + lax.broadcasted_iota(
-        jnp.int32, (padded_n, slots), 1
-    )
-
-    def shift(x, bit):
-        if bit < lane_bits:
-            amount = 1 << bit
-            rolled = pltpu.roll(x, slots - amount, 1)
-            after = jnp.concatenate([rolled[ROWS:], rolled[:ROWS]], axis=0)
-            lanes = lax.broadcasted_iota(jnp.int32, x.shape, 1)
-            return jnp.where(lanes < slots - amount, rolled, after)
-        cut = ROWS << (bit - lane_bits)
-        return jnp.concatenate([x[cut:], x[:cut]], axis=0)
+    for bit in range(lane_bits):
+        near = pltpu.roll(left, slots - (1 << bit), 1)
+        take = (near & (1 << bit)) != 0
+        leaves = (left & (1 << bit)) != 0
+        left = jnp.where(take, near, jnp.where(leaves, 0, left))
+    source = lanes + left
+    for bit in range(lane_bits):
+        source = jnp.where((start & (1 << bit)) != 0, pltpu.roll(source, 1 << bit, 1), source)
+    offset = (lanes - start) & (slots - 1)
+    sources[...] = source & (slots - 1)
+    places[...] = jnp.where(offset < inside, (start + offset) >> lane_bits, -1)
+    ends = start + inside
+    for t in range(tiles):
+        last = t * padded_n + n - 1
+        limits[0, t] = jnp.max(ends[last : last + 1])
+        own_x = all_ref[1, 1 + t // out_z, gz * out_z + t % out_z, pl.ds(0, 1), :]
+        limits[1, t] = jnp.sum(jnp.where(own_x < 0.5 * FAR, 1.0, 0.0)).astype(jnp.int32)
 
     def one_tile(tile, carry):
-        y = tile // out_z
-        zz = tile % out_z
+        y, zz = tile // out_z, tile % out_z
         z = gz * out_z + zz
         own = all_ref[1, y + 1, z]
-        pieces, masks = [], []
-        for dx, dy, dz in shell:
-            if dz is None:
-                v = all_ref[1 + dx, y + 1 + dy, 1 - z]
-                shift_z = jnp.where(v < 0.5 * SIDE, SIDE, -SIDE)
-            else:
-                v = all_ref[1 + dx, y + 1 + dy, lax.rem(z + dz + tiles_z, tiles_z)]
-                shift_z = SIDE * dz
-            move = jnp.where(row == 0, SIDE * dx, jnp.where(row == 1, SIDE * dy, jnp.where(row == 2, shift_z, 0.0)))
-            v = v + move
-            inside = jnp.where((v > low) & (v < high), 1.0, 0.0)
-            masks.append(jnp.min(inside, axis=0, keepdims=True))
-            pieces.append(v)
-        masks += [jnp.zeros((1, slots), jnp.float32)] * (padded_n - n)
-        mask = jnp.concatenate(masks, axis=0)
-        half = mask.astype(jnp.bfloat16)
-        before = jnp.dot(half, upper, preferred_element_type=jnp.float32)
-        per_row = jnp.sum(mask, axis=1, keepdims=True)
-        rows_before = jnp.dot(
-            below,
-            jnp.broadcast_to(per_row, (padded_n, slots)).astype(jnp.bfloat16),
-            preferred_element_type=jnp.float32,
-        )
-        total = jnp.sum(mask).astype(jnp.int32)
-        distance_left = jnp.where(mask > 0.5, flat - (before + rows_before).astype(jnp.int32), 0)
-        x = jnp.concatenate(pieces, axis=0)
-        s = jnp.concatenate(
-            [jnp.broadcast_to(distance_left[k : k + 1], (ROWS, slots)) for k in range(n)], axis=0
-        )
-        for bit in range(bits):
-            near = shift(s, bit)
-            take = (near & (1 << bit)) != 0
-            leaves = (s & (1 << bit)) != 0
-            x = jnp.where(take, shift(x, bit), x)
-            s = jnp.where(take, near, jnp.where(leaves, 0, s))
+        first = tile * padded_n
+        for k in range(n):
+            index = jnp.broadcast_to(sources[pl.ds(first + k, 1), :], (ROWS, slots))
+            moved[k] = jnp.take_along_axis(candidate(k, y, z), index, axis=1, mode="promise_in_bounds")
+        blocks = 1 + (limits[0, tile] + slots - 1) // slots
+        count = limits[1, tile]
         jbuf[0] = own
-        for k in range(n):
-            jbuf[1 + k] = jnp.where(lane + k * slots < total, x[k * ROWS : (k + 1) * ROWS], FAR)
-        blocks = 1 + (total + slots - 1) // slots
-
+
+        def fill(b, carry):
+            block = jnp.full((ROWS, slots), FAR, jnp.float32)
+            for k in range(n):
+                block = jnp.where(places[pl.ds(first + k, 1), :] == b - 1, moved[k], block)
+            jbuf[b] = block
+            return carry
+
+        lax.fori_loop(1, blocks, fill, 0)
         column[:, :ROWS] = jnp.transpose(own)
-        count = jnp.sum(jnp.where(own[0:1] < 0.5 * FAR, 1.0, 0.0)).astype(jnp.int32)
         groups = (count + GROUP - 1) // GROUP
 
         def one_group(g, carry):
@@ -266,7 +284,7 @@
             out_ref[c, 0, y, pl.ds(zz, 1), :] = kick[c : c + 1]
         return carry
 
-    lax.fori_loop(0, out_y * out_z, one_tile, 0)
+    lax.fori_loop(0, tiles, one_tile, 0)
 
 
 def on_device(nx, ny, nz, positions, velocities, bead_keys, counts):
@@ -288,8 +306,9 @@
         ],
         compiler_params=pltpu.CompilerParams(collective_id=0, has_side_effects=True),
         name="gather_tiles",
-    )(positions, velocities, bead_keys, counts)
-    shells = 17 if tiles_z == 2 else 26
+    )(positions, velocities, bead_keys, jnp.swapaxes(counts, 1, 2))
+    shells = len(shell_of(tiles_z))
+    height = out_y * out_z * (-(-shells // 8) * 8)
     return pl.pallas_call(
         functools.partial(pair_kernel, (tiles_z, out_y, out_z)),
         out_shape=jax.ShapeDtypeStruct((3, 1, out_y, out_z, slots), jnp.float32),
@@ -299,6 +318,11 @@
             pltpu.VMEM((1 + shells, ROWS, slots), jnp.float32),
             pltpu.VMEM((slots, slots), jnp.float32),
             pltpu.VMEM((slots, slots), jnp.float32),
+            pltpu.VMEM((height, slots), jnp.float32),
+            pltpu.VMEM((height, slots), jnp.int32),
+            pltpu.VMEM((height, slots), jnp.int32),
+            pltpu.VMEM((shells, ROWS, slots), jnp.float32),
+            pltpu.SMEM((2, out_y * out_z), jnp.int32),
         ],
         name="pair_kicks",
     )(gathered)

time: 31.1 us -> 26.3 us (0.85); the launches traced: 31 us -> 25.8 us
  Pallas kernels: 29.7 us -> 25.8 us
  local copies, waits for them, and re-layouts: 1.34 us -> 0 us
    pallas_call x1, Pallas kernels: 18.2 us -> 14.3 us  [on_device(): pl.pallas_call(functools.partial(pair_kernel, (tiles_z, out_y, out_z)), o...]
    unnamed x1 -> x0, local copies, waits for them, and re-layouts: 1.34 us -> none
where the time goes in v2:
time: 26.3 us; the launch traced here: 25.8 us
  Pallas kernels  25.8 us (98%)
    pallas_call x1, Pallas kernels, on_device(): pl.pallas_call(functools.partial(pair_kernel, (tiles_z, out_y, out_z)), o...  14.3 us
    pallas_call x1, Pallas kernels, on_device(): pl.pallas_call(functools.partial(gather_kernel, (nx, ny, nz, block_y, til...  11.4 us

profile of v2, /device:TPU:0, one launch (start us, length us, event | category | flops | bytes accessed | tf_op | source)
XLA Modules:
  0.0 25.8 jit_solution(1631212163538449356)
XLA Ops:
  0.0 11.4 %gather_tiles.1.all_ref = f32[3,10,2,8,128]{4,3,2,1,0:T(8,128)} custom-call(f32[3,1,4,2,128]{4,3,2,1,0:T(2,128)} %pos_ref.1, f32[3,1,4,2,128]{4,3,2,1,0:T(2,128)} %vel_ref.1, s32[1,4,2,128]{3,2,1,0:T(2,128)} %key_ref.1, s32[1,2,4]{2,1,0:T(2,128)} %bitcast.1), custom_call_target="tpu_custom_call" | custom-call | tf_op jit(solution)/shard_map/gather_tiles/pallas_call | solution.py:294
  11.4 14.3 %pair_kicks.1 = f32[3,1,8,1,128]{4,3,2,1,0:T(1,128)} custom-call(f32[3,10,2,8,128]{4,3,2,1,0:T(8,128)} %gather_tiles.1.all_ref), custom_call_target="tpu_custom_call" | custom-call | tf_op jit(solution)/shard_map/pair_kicks/pallas_call | solution.py:312

commit v3 on v2

--- a/solution.py
+++ b/solution.py
@@ -19,14 +19,18 @@
 
 FAR = 1.0e9
 ROWS = 8
-GROUP = 64
+GROUP = 128
 MESH = pl.DeviceIdType.MESH
 
 
-def gather_kernel(sizes, pos_ref, vel_ref, key_ref, count_ref, all_ref, packed, send, recv, edge_send, edge_recv, local):
+def gather_kernel(sizes, pos_in, vel_in, key_in, count_in, all_ref, pos_ref, vel_ref, key_ref, count_ref, packed, send, recv, edge_send, edge_recv, local, loads):
     nx, ny, nz, block_y, tiles_z = sizes
     gx, gy, gz = lax.axis_index("gx"), lax.axis_index("gy"), lax.axis_index("gz")
     slots = pos_ref.shape[-1]
+    inputs = ((pos_in, pos_ref), (vel_in, vel_ref), (key_in, key_ref), (count_in, count_ref))
+    fetches = [pltpu.make_async_copy(a, b, loads.at[k]) for k, (a, b) in enumerate(inputs)]
+    for fetch in fetches:
+        fetch.start()
     top = nz * block_y + 1
     barrier = pltpu.get_barrier_semaphore()
 
@@ -41,6 +45,8 @@
         pl.semaphore_signal(barrier, inc=1, device_id=target(e, -1, nz - 1), device_id_type=MESH)
         pl.semaphore_signal(barrier, inc=1, device_id=target(e, 1, 0), device_id_type=MESH)
 
+    for fetch in fetches:
+        fetch.wait()
     lane = lax.broadcasted_iota(jnp.int32, (1, slots), 1)
     for y in range(block_y):
         for z in range(tiles_z):
@@ -156,7 +162,7 @@
         masks[pl.ds(pl.multiple_of(tile * padded_n, 8), padded_n), :] = jnp.concatenate(rows, axis=0)
         return carry
 
-    lax.fori_loop(0, tiles, mark, 0)
+    lax.fori_loop(0, tiles, mark, 0, unroll=2)
 
     def square(size, test):
         i = lax.broadcasted_iota(jnp.int32, (size, size), 0)
@@ -201,14 +207,22 @@
         own_x = all_ref[1, 1 + t // out_z, gz * out_z + t % out_z, pl.ds(0, 1), :]
         limits[1, t] = jnp.sum(jnp.where(own_x < 0.5 * FAR, 1.0, 0.0)).astype(jnp.int32)
 
+    def collect(tile, carry):
+        y, z = tile // out_z, gz * out_z + tile % out_z
+        first = tile * padded_n
+        for k in range(n):
+            index = jnp.broadcast_to(sources[pl.ds(first + k, 1), :], (ROWS, slots))
+            moved[tile, k] = jnp.take_along_axis(candidate(k, y, z), index, axis=1, mode="promise_in_bounds")
+        column[tile, :, :ROWS] = jnp.transpose(all_ref[1, y + 1, z])
+        return carry
+
+    lax.fori_loop(0, tiles, collect, 0, unroll=2)
+
     def one_tile(tile, carry):
         y, zz = tile // out_z, tile % out_z
         z = gz * out_z + zz
         own = all_ref[1, y + 1, z]
         first = tile * padded_n
-        for k in range(n):
-            index = jnp.broadcast_to(sources[pl.ds(first + k, 1), :], (ROWS, slots))
-            moved[k] = jnp.take_along_axis(candidate(k, y, z), index, axis=1, mode="promise_in_bounds")
         blocks = 1 + (limits[0, tile] + slots - 1) // slots
         count = limits[1, tile]
         jbuf[0] = own
@@ -216,19 +230,18 @@
         def fill(b, carry):
             block = jnp.full((ROWS, slots), FAR, jnp.float32)
             for k in range(n):
-                block = jnp.where(places[pl.ds(first + k, 1), :] == b - 1, moved[k], block)
+                block = jnp.where(places[pl.ds(first + k, 1), :] == b - 1, moved[tile, k], block)
             jbuf[b] = block
             return carry
 
         lax.fori_loop(1, blocks, fill, 0)
-        column[:, :ROWS] = jnp.transpose(own)
         groups = (count + GROUP - 1) // GROUP
 
         def one_group(g, carry):
             base = pl.multiple_of(g * GROUP, GROUP)
 
             def wide(c):
-                return jnp.broadcast_to(column[pl.ds(base, GROUP), c : c + 1], (GROUP, slots))
+                return jnp.broadcast_to(column[tile, pl.ds(base, GROUP), c : c + 1], (GROUP, slots))
 
             xi = [wide(c) for c in range(6)]
             klo = wide(7).astype(jnp.int32)
@@ -242,8 +255,9 @@
 
                 sep = [xi[c] - other(c) for c in range(3)]
                 squared = sep[0] * sep[0] + sep[1] * sep[1] + sep[2] * sep[2]
-                distance = squared * lax.rsqrt(jnp.maximum(squared, 1e-30))
-                inverse = lax.rsqrt(jnp.maximum(squared, soft_radius * soft_radius))
+                root = lax.rsqrt(jnp.maximum(squared, 1e-30))
+                distance = squared * root
+                inverse = jnp.minimum(root, 1.0 / soft_radius)
                 weight = jnp.maximum(1.0 - distance, 0.0)
                 dot = (
                     sep[0] * (xi[3] - other(3))
@@ -270,21 +284,25 @@
 
             zero = jnp.zeros((GROUP, slots), jnp.float32)
             acc = lax.fori_loop(0, blocks, one_block, (zero, zero, zero))
-            lanes = lax.broadcasted_iota(jnp.int32, (GROUP, slots), 1)
-            sums = [jnp.sum(a, axis=1, keepdims=True) for a in acc]
-            forces[pl.ds(base, GROUP), :] = jnp.where(
-                lanes == 0, sums[0], jnp.where(lanes == 1, sums[1], sums[2])
-            )
+            for c in range(3):
+                forces[tile, c, pl.ds(base, GROUP), :] = acc[c]
             return carry
 
         lax.fori_loop(0, groups, one_group, 0)
-        turned = jnp.transpose(forces[...])
-        kick = jnp.where(lane[:3] < count, kick_scale * turned[:3], 0.0)
+        return carry
+
+    lax.fori_loop(0, tiles, one_tile, 0)
+
+    def finish(tile, carry):
+        lanes = lax.broadcasted_iota(jnp.int32, (slots, slots), 1)
+        sums = [jnp.sum(forces[tile, c], axis=1, keepdims=True) for c in range(3)]
+        turned = jnp.transpose(jnp.where(lanes == 0, sums[0], jnp.where(lanes == 1, sums[1], sums[2])))
+        kick = jnp.where(lane[:3] < limits[1, tile], kick_scale * turned[:3], 0.0)
         for c in range(3):
-            out_ref[c, 0, y, pl.ds(zz, 1), :] = kick[c : c + 1]
+            out_ref[c, 0, tile // out_z, pl.ds(tile % out_z, 1), :] = kick[c : c + 1]
         return carry
 
-    lax.fori_loop(0, tiles, one_tile, 0)
+    lax.fori_loop(0, tiles, finish, 0, unroll=2)
 
 
 def on_device(nx, ny, nz, positions, velocities, bead_keys, counts):
@@ -294,17 +312,24 @@
     gathered = pl.pallas_call(
         functools.partial(gather_kernel, (nx, ny, nz, block_y, tiles_z)),
         out_shape=jax.ShapeDtypeStruct((3, span, tiles_z, ROWS, slots), jnp.float32),
-        in_specs=[pl.BlockSpec(memory_space=pltpu.VMEM)] * 3 + [pl.BlockSpec(memory_space=pltpu.SMEM)],
-        out_specs=pl.BlockSpec(memory_space=pltpu.VMEM),
+        in_specs=[pl.BlockSpec(memory_space=pltpu.HBM)] * 4,
+        out_specs=pl.BlockSpec(memory_space=pl.ANY),
         scratch_shapes=[
+            pltpu.VMEM(positions.shape, jnp.float32),
+            pltpu.VMEM(velocities.shape, jnp.float32),
+            pltpu.VMEM(bead_keys.shape, jnp.int32),
+            pltpu.SMEM((1, tiles_z, block_y), jnp.int32),
             pltpu.VMEM((block_y, tiles_z, ROWS, slots), jnp.float32),
             pltpu.SemaphoreType.DMA((3, nz)),
             pltpu.SemaphoreType.DMA((3, nz)),
             pltpu.SemaphoreType.DMA((2, 3, nz)),
             pltpu.SemaphoreType.DMA((2, 3)),
             pltpu.SemaphoreType.DMA,
+            pltpu.SemaphoreType.DMA((4,)),
         ],
-        compiler_params=pltpu.CompilerParams(collective_id=0, has_side_effects=True),
+        compiler_params=pltpu.CompilerParams(
+            collective_id=0, has_side_effects=True, vmem_limit_bytes=8 << 20
+        ),
         name="gather_tiles",
     )(positions, velocities, bead_keys, jnp.swapaxes(counts, 1, 2))
     shells = len(shell_of(tiles_z))
@@ -316,14 +341,15 @@
         out_specs=pl.BlockSpec(memory_space=pltpu.VMEM),
         scratch_shapes=[
             pltpu.VMEM((1 + shells, ROWS, slots), jnp.float32),
-            pltpu.VMEM((slots, slots), jnp.float32),
-            pltpu.VMEM((slots, slots), jnp.float32),
+            pltpu.VMEM((out_y * out_z, slots, slots), jnp.float32),
+            pltpu.VMEM((out_y * out_z, 3, slots, slots), jnp.float32),
             pltpu.VMEM((height, slots), jnp.float32),
             pltpu.VMEM((height, slots), jnp.int32),
             pltpu.VMEM((height, slots), jnp.int32),
-            pltpu.VMEM((shells, ROWS, slots), jnp.float32),
+            pltpu.VMEM((out_y * out_z, shells, ROWS, slots), jnp.float32),
             pltpu.SMEM((2, out_y * out_z), jnp.int32),
         ],
+        compiler_params=pltpu.CompilerParams(vmem_limit_bytes=8 << 20),
         name="pair_kicks",
     )(gathered)
 

time: 26.3 us -> 24.8 us (0.943); the launches traced: 25.8 us -> 25 us
  Pallas kernels: 25.8 us -> 22.2 us
  local copies, waits for them, and re-layouts: 0 us -> 2.78 us
    unnamed x0 -> x8, local copies, waits for them, and re-layouts: none -> 2.78 us
    pallas_call x1, Pallas kernels: 14.3 us -> 12.2 us  [on_device(): pl.pallas_call(functools.partial(pair_kernel, (tiles_z, out_y, out_z)), o...]
    pallas_call x1, Pallas kernels: 11.4 us -> 9.96 us  [on_device(): pl.pallas_call(functools.partial(gather_kernel, (nx, ny, nz, block_y, til...]
where the time goes in v3:
time: 24.8 us; the launch traced here: 25 us
  Pallas kernels  22.2 us (90%)
  local copies, waits for them, and re-layouts  2.78 us (11%)
    pallas_call x1, Pallas kernels, on_device(): pl.pallas_call(functools.partial(pair_kernel, (tiles_z, out_y, out_z)), o...  12.2 us
    pallas_call x1, Pallas kernels, on_device(): pl.pallas_call(functools.partial(gather_kernel, (nx, ny, nz, block_y, til...  9.96 us
    unnamed x8, local copies, waits for them, and re-layouts  2.78 us

profile of v3, /device:TPU:0, one launch (start us, length us, event | category | flops | bytes accessed | tf_op | source)
XLA Modules:
  0.0 25.0 jit_solution(14335804932154673305)
XLA Ops:
  0.0 0.0 copy-start.3
  0.0 0.7 %copy-done.3 = s32[1,4,2]{1,2,0:T(2,128)S(1)} copy-done((s32[1,4,2]{1,2,0:T(2,128)S(1)}, s32[1,4,2]{1,2,0:T(2,128)}, u32[]{:S(2)}) %copy-start.3) | copy-done | bytes 56
  0.7 0.0 copy-start
  0.7 0.7 %copy-done = f32[3,1,4,2,128]{4,3,2,1,0:T(2,128)S(1)} copy-done((f32[3,1,4,2,128]{4,3,2,1,0:T(2,128)S(1)}, f32[3,1,4,2,128]{4,3,2,1,0:T(2,128)}, u32[]{:S(2)}) %copy-start) | copy-done | bytes 12312
  1.4 0.0 copy-start.1
  1.4 0.7 %copy-done.1 = f32[3,1,4,2,128]{4,3,2,1,0:T(2,128)S(1)} copy-done((f32[3,1,4,2,128]{4,3,2,1,0:T(2,128)S(1)}, f32[3,1,4,2,128]{4,3,2,1,0:T(2,128)}, u32[]{:S(2)}) %copy-start.1) | copy-done | bytes 12312
  2.1 0.0 copy-start.2
  2.1 0.7 %copy-done.2 = s32[1,4,2,128]{3,2,1,0:T(2,128)S(1)} copy-done((s32[1,4,2,128]{3,2,1,0:T(2,128)S(1)}, s32[1,4,2,128]{3,2,1,0:T(2,128)}, u32[]{:S(2)}) %copy-start.2) | copy-done | bytes 4120
  2.8 10.0 %gather_tiles.1.all_ref = f32[3,10,2,8,128]{4,3,2,1,0:T(8,128)S(1)} custom-call(f32[3,1,4,2,128]{4,3,2,1,0:T(2,128)S(1)} %copy-done, f32[3,1,4,2,128]{4,3,2,1,0:T(2,128)S(1)} %copy-done.1, s32[1,4,2,128]{3,2,1,0:T(2,128)S(1)} %copy-done.2, s32[1,2,4]{2,1,0:T(2,128)S(1)} %bitcast.1), custom_call_target="tpu_custom_call" | custom-call | tf_op jit(solution)/shard_map/gather_tiles/pallas_call | solution.py:312
  12.7 12.2 %pair_kicks.1 = f32[3,1,8,1,128]{4,3,2,1,0:T(1,128)} custom-call(f32[3,10,2,8,128]{4,3,2,1,0:T(8,128)S(1)} %gather_tiles.1.all_ref), custom_call_target="tpu_custom_call" | custom-call | tf_op jit(solution)/shard_map/pair_kicks/pallas_call | solution.py:337
Async XLA Ops:
  0.0 0.7 %copy-start.3 = (s32[1,4,2]{1,2,0:T(2,128)S(1)}, s32[1,4,2]{1,2,0:T(2,128)}, u32[]{:S(2)}) copy-start(s32[1,4,2]{1,2,0:T(2,128)} %param.7) | copy-start | bytes 100
  0.7 0.7 %copy-start = (f32[3,1,4,2,128]{4,3,2,1,0:T(2,128)S(1)}, f32[3,1,4,2,128]{4,3,2,1,0:T(2,128)}, u32[]{:S(2)}) copy-start(f32[3,1,4,2,128]{4,3,2,1,0:T(2,128)} %pos_in.1) | copy-start | bytes 36868
  1.4 0.7 %copy-start.1 = (f32[3,1,4,2,128]{4,3,2,1,0:T(2,128)S(1)}, f32[3,1,4,2,128]{4,3,2,1,0:T(2,128)}, u32[]{:S(2)}) copy-start(f32[3,1,4,2,128]{4,3,2,1,0:T(2,128)} %vel_in.1) | copy-start | bytes 36868
  2.1 0.7 %copy-start.2 = (s32[1,4,2,128]{3,2,1,0:T(2,128)S(1)}, s32[1,4,2,128]{3,2,1,0:T(2,128)}, u32[]{:S(2)}) copy-start(s32[1,4,2,128]{3,2,1,0:T(2,128)} %key_in.1) | copy-start | bytes 12292

commit v4 on v3

--- a/solution.py
+++ b/solution.py
@@ -328,7 +328,7 @@
             pltpu.SemaphoreType.DMA((4,)),
         ],
         compiler_params=pltpu.CompilerParams(
-            collective_id=0, has_side_effects=True, vmem_limit_bytes=8 << 20
+            collective_id=0, has_side_effects=True
         ),
         name="gather_tiles",
     )(positions, velocities, bead_keys, jnp.swapaxes(counts, 1, 2))
@@ -349,7 +349,6 @@
             pltpu.VMEM((out_y * out_z, shells, ROWS, slots), jnp.float32),
             pltpu.SMEM((2, out_y * out_z), jnp.int32),
         ],
-        compiler_params=pltpu.CompilerParams(vmem_limit_bytes=8 << 20),
         name="pair_kicks",
     )(gathered)
 

time: 24.8 us -> 22.9 us (0.923)
  the two profiles are of different devices: /device:TPU:0 before, /device:TPU:3 now
where the time goes in v4:
time: 22.9 us; the launch traced here: 22.5 us
  Pallas kernels  22.5 us (98%)
    pallas_call x1, Pallas kernels, on_device(): pl.pallas_call(functools.partial(pair_kernel, (tiles_z, out_y, out_z)), o...  12.7 us
    pallas_call x1, Pallas kernels, on_device(): pl.pallas_call(functools.partial(gather_kernel, (nx, ny, nz, block_y, til...  9.76 us

profile of v4, /device:TPU:3, one launch (start us, length us, event | category | flops | bytes accessed | tf_op | source)
XLA Modules:
  0.0 22.5 jit_solution(16861305758923415763)
XLA Ops:
  0.0 9.8 %gather_tiles.1.all_ref = f32[3,10,2,8,128]{4,3,2,1,0:T(8,128)} custom-call(f32[3,1,4,2,128]{4,3,2,1,0:T(2,128)} %pos_in.1, f32[3,1,4,2,128]{4,3,2,1,0:T(2,128)} %vel_in.1, s32[1,4,2,128]{3,2,1,0:T(2,128)} %key_in.1, s32[1,2,4]{2,1,0:T(2,128)} %bitcast.1), custom_call_target="tpu_custom_call" | custom-call | tf_op jit(solution)/shard_map/gather_tiles/pallas_call | solution.py:312
  9.8 12.7 %pair_kicks.1 = f32[3,1,8,1,128]{4,3,2,1,0:T(1,128)} custom-call(f32[3,10,2,8,128]{4,3,2,1,0:T(8,128)} %gather_tiles.1.all_ref), custom_call_target="tpu_custom_call" | custom-call | tf_op jit(solution)/shard_map/pair_kicks/pallas_call | solution.py:337
